TPU v7x, 32 devices: a whole 2x2x4 slice. The times are simulated.
32 devices in a mesh: seq: 8 (over z, x), res: 4 (over y, core).
Axes of the slice: x: 2, y: 2, z: 4, core: 2. Of those that a mesh axis runs over, the one named last changes fastest.
Arguments:
- alignment: bfloat16 [128, 4, 128, 256], P('seq', 'res'), may hold values from -8 to 8
- gain_attn: float32 [256], replicated, may hold values from 0.1 to 1.9
- w_proj: bfloat16 [256, 4, 256], replicated, may hold values from -0.75 to 0.75
- w_out: bfloat16 [256, 256], replicated, may hold values from -0.375 to 0.375
- gain_head: float32 [256], replicated, may hold values from 0.1 to 1.9
- w_head: bfloat16 [256, 23], replicated, may hold values from -1 to 1
- masked: int32 [128, 4, 128], P('res', None, 'seq'), may hold values from 0 to 1
- labels: int32 [128, 4, 128], P('res', None, 'seq'), may hold values from 0 to 22
Outputs:
- updated: bfloat16 [128, 4, 128, 256], P('res', None, 'seq')
- masked_loss: float32 [], replicated
- mask_share: float32 [], replicated
All inputs are finite; a program needn't handle non-finite values.
Results may differ from a plain program's by a relative error of at most 0.011.
Values may be sent and summed in bfloat16 or wider, within the bound.
A program may use at most 192 MiB of HBM per device.

v0:
```python
import jax
import jax.numpy as jnp
from jax import lax
from jax.sharding import PartitionSpec as P

HEADS = 8
HEAD_DIM = 32


def normalize(values, gain):
    mean = jnp.mean(values, axis=-1, keepdims=True)
    centred = values - mean
    spread = jnp.mean(centred * centred, axis=-1, keepdims=True)
    return centred * lax.rsqrt(spread + 1e-05) * gain


def project(flat_rows, gain_attn, w_proj):
    features = flat_rows.shape[1]
    normed = normalize(flat_rows.astype(jnp.float32), gain_attn).astype(jnp.bfloat16)
    return jnp.dot(
        normed, w_proj.reshape(features, 4 * features), preferred_element_type=jnp.float32
    ).astype(jnp.bfloat16)


def column_attention(queries, key_part, value_part):
    inv_root = HEAD_DIM ** (-0.5)
    scores = (
        jnp.einsum("shd,thd->hst", queries, key_part, preferred_element_type=jnp.float32) * inv_root
    )
    probs = jnp.exp(scores)
    totals = jnp.sum(probs, axis=2)
    weighted = jnp.einsum(
        "hst,thd->shd", probs.astype(jnp.bfloat16), value_part, preferred_element_type=jnp.float32
    )
    return (weighted, totals)


def finish(flat_rows, gated, w_out):
    summed = flat_rows.astype(jnp.float32) + jnp.dot(
        gated, w_out, preferred_element_type=jnp.float32
    )
    return summed.astype(jnp.bfloat16)


def on_device(alignment, gain_attn, w_proj, w_out, gain_head, w_head, masked, labels):
    weights = masked.reshape(-1).astype(jnp.float32)
    local_count = jnp.sum(weights)
    local_rows, single_block, segment, features = alignment.shape
    seq_devices = lax.axis_size("seq")
    split_view = alignment.reshape(local_rows, seq_devices, segment // seq_devices, features)
    column_block = lax.all_to_all(split_view, "seq", split_axis=1, concat_axis=0, tiled=True)
    seq_total, single, col_count, features = column_block.shape
    by_column = jnp.transpose(column_block.reshape(seq_total, col_count, features), (1, 0, 2))
    flat_rows = by_column.reshape(col_count * seq_total, features)
    projected = project(flat_rows, gain_attn, w_proj).reshape(
        col_count, seq_total, 4, HEADS, HEAD_DIM
    )

    def per_column(picked):
        weighted, totals = column_attention(picked[:, 0], picked[:, 1], picked[:, 2])
        attended = weighted / totals.T[:, :, None]
        gated_col = attended * jax.nn.sigmoid(picked[:, 3].astype(jnp.float32))
        return gated_col.reshape(seq_total, features).astype(jnp.bfloat16)

    gated = lax.map(per_column, projected).reshape(col_count * seq_total, features)
    result = finish(flat_rows, gated, w_out).reshape(col_count, seq_total, features)
    result = jnp.transpose(result, (1, 0, 2)).reshape(seq_total, single, col_count, features)
    updated = lax.all_to_all(result, "res", split_axis=0, concat_axis=1, tiled=True)
    features = updated.shape[3]
    flat_out = updated.reshape(-1, features)
    head_in = normalize(flat_out.astype(jnp.float32), gain_head).astype(jnp.bfloat16)
    logits = jnp.einsum("rc,ck->kr", head_in, w_head, preferred_element_type=jnp.float32)
    log_total = jnp.log(jnp.sum(jnp.exp(logits), axis=0))
    classes = jnp.arange(logits.shape[0], dtype=jnp.int32)[:, None]
    picked = jnp.sum(jnp.where(classes == labels.reshape(1, -1), logits, 0.0), axis=0)
    errors = log_total - picked
    local_loss = jnp.sum(errors * weights)
    loss_sum, mask_count = lax.psum((local_loss, local_count), ("seq", "res"))
    entries = flat_out.shape[0] * lax.axis_size("seq") * lax.axis_size("res")
    masked_loss = loss_sum / (1.0 + mask_count)
    mask_share = mask_count / entries
    return (updated, masked_loss, mask_share)


def solution(mesh):
    in_specs = (
        P("seq", "res", None, None),
        P(),
        P(),
        P(),
        P(),
        P(),
        P("res", None, "seq"),
        P("res", None, "seq"),
    )
    out_specs = (P("res", None, "seq", None), P(), P())
    return jax.shard_map(
        on_device, mesh=mesh, in_specs=in_specs, out_specs=out_specs, check_vma=False
    )
```

profile of v0, /device:TPU:0, one launch (start us, length us, event | category | flops | bytes accessed | tf_op | source)
XLA Modules:
  0.0 151.8 jit_solution(10787070603162363327)
XLA Ops:
  0.7 2.4 %copy.61 = bf16[16,8,16,256]{3,2,0,1:T(8,128)(2,1)} copy(bf16[16,8,16,256]{3,2,1,0:T(8,128)(2,1)} %bitcast.113) | data formatting | bytes 2097152 | tf_op jit(solution)/shard_map/reshape | solution.py:50
  3.0 7.3 %all-to-all-start = ((bf16[16,8,16,256]{3,2,0,1:T(8,128)(2,1)}), bf16[16,8,16,256]{3,2,0,1:T(8,128)(2,1)S(1)}, u32[]{:S(2)}, u32[]{:S(2)}) async-start(bf16[16,8,16,256]{3,2,0,1:T(8,128)(2,1)} %copy.61), calls=%async_computation | async-start | bytes 2097152 | tf_op jit(solution)/shard_map/all_to_all | solution.py:51
  10.4 25.7 %all-to-all-done = bf16[16,8,16,256]{3,2,0,1:T(8,128)(2,1)S(1)} async-done(((bf16[16,8,16,256]{3,2,0,1:T(8,128)(2,1)}), bf16[16,8,16,256]{3,2,0,1:T(8,128)(2,1)S(1)}, u32[]{:S(2)}, u32[]{:S(2)}) %all-to-all-start) | async-done | bytes 1048608 | tf_op jit(solution)/shard_map/all_to_all | solution.py:51
  36.3 1.2 bitcast_reduce_fusion
  37.5 1.2 copy.62
  38.8 1.6 %multiply_reduce_fusion.1 = f32[16,128]{1,0:T(8,128)S(1)} fusion(f32[16,128]{1,0:T(8,128)S(1)} %broadcast_multiply_fusion.1, f32[128,16,256]{2,1,0:T(8,128)S(1)} %bitcast.100), kind=kLoop, calls=%fused_computation.24 | loop fusion | flops 1570816 | bytes 2113536 | tf_op jit(solution)/shard_map/reduce_sum | solution.py:13
  40.4 1.4 multiply_convert_fusion
  41.8 3.2 %convolution_convert_fusion = bf16[2048,1024]{1,0:T(8,128)(2,1)} fusion(bf16[2048,256]{1,0:T(8,128)(2,1)S(1)} %bitcast.109, bf16[256,1024]{1,0:T(8,128)(2,1)S(1)} %bitcast.111), kind=kOutput, calls=%fused_computation.12 | convolution fusion | flops 1075838976 | bytes 5767168 | tf_op jit(solution)/shard_map/dot_general | solution.py:20
  45.0 6.5 %copy.63 = bf16[2048,1024]{0,1:T(8,128)(2,1)} copy(bf16[2048,1024]{1,0:T(8,128)(2,1)} %convolution_convert_fusion) | data formatting | bytes 8388608 | tf_op jit(solution)/shard_map/convert_element_type | solution.py:22
  51.5 3.6 %copy.80 = bf16[128,8,16,128]{3,2,1,0:T(8,128)(2,1)S(1)} copy(bf16[128,8,16,128]{3,1,2,0:T(8,128)(2,1)} %bitcast.106) | data formatting | bytes 8388608
  55.1 3.0 %copy.64 = bf16[16,128,4,8,32]{1,4,3,2,0:T(8,128)(2,1)} copy(bf16[16,128,4,8,32]{1,0,4,3,2:T(8,128)(2,1)S(1)} %bitcast.107) | data formatting | bytes 8388608 | tf_op jit(solution)/shard_map/while | solution.py:65
  58.1 26.1 %while.10 = (s32[]{:T(128)}, bf16[16,128,256]{2,1,0:T(8,128)(2,1)S(1)}, bf16[16,128,4,8,32]{1,4,3,2,0:T(8,128)(2,1)}, s32[]{:T(128)}) while((s32[]{:T(128)}, bf16[16,128,256]{2,1,0:T(8,128)(2,1)S(1)}, bf16[16,128,4,8,32]{1,4,3,2,0:T(8,128)(2,1)}, s32[]{:T(128)}) %tuple.42), condition=%wide.region_4.0_spmd, body=%wide.region_2.4_spmd.sunk | while | flops 17398784 | bytes 1646653 | solution.py:65
  59.7 1.0 dynamic-slice_bitcast_fusion.2
  61.4 1.0 dynamic-slice_bitcast_fusion.2
  69.5 1.0 dynamic-slice_bitcast_fusion.2
  72.8 1.0 dynamic-slice_bitcast_fusion.2
  74.4 1.0 dynamic-slice_bitcast_fusion.2
  81.0 1.0 dynamic-slice_bitcast_fusion.2
  84.7 1.6 %copy.85 = bf16[16,128,256]{2,0,1:T(8,128)(2,1)} copy(bf16[16,128,256]{2,1,0:T(8,128)(2,1)S(1)} %bitcast.110) | data formatting | bytes 2097152 | tf_op jit(solution)/shard_map/reshape | solution.py:66
  86.3 3.7 %all-to-all-start.1 = ((bf16[128,1,16,256]{3,2,1,0:T(8,128)(2,1)}), bf16[128,1,16,256]{3,2,1,0:T(8,128)(2,1)S(1)}, u32[]{:S(2)}, u32[]{:S(2)}) async-start(bf16[128,1,16,256]{3,2,1,0:T(8,128)(2,1)} %bitcast.79), calls=%async_computation.1 | async-start | bytes 2097152 | tf_op jit(solution)/shard_map/all_to_all | solution.py:68
  90.3 13.9 %all-to-all-done.1 = bf16[128,1,16,256]{3,2,1,0:T(8,128)(2,1)S(1)} async-done(((bf16[128,1,16,256]{3,2,1,0:T(8,128)(2,1)}), bf16[128,1,16,256]{3,2,1,0:T(8,128)(2,1)S(1)}, u32[]{:S(2)}, u32[]{:S(2)}) %all-to-all-start.1) | async-done | bytes 1048608 | tf_op jit(solution)/shard_map/all_to_all | solution.py:68
  107.1 1.1 exponential_reduce_fusion
  109.0 37.5 %all-reduce = (f32[]{:T(128)}, f32[]{:T(128)}) all-reduce(f32[]{:T(128)} %get-tuple-element.57, f32[]{:T(128)} %get-tuple-element.56), channel_id=1, replica_groups=mesh['seq'=8,'res'=4] {'seq','res'}, use_global_device_ids=true, to_apply=%region_10.11 | all-reduce | flops 2 | bytes 16 | tf_op jit(solution)/shard_map/psum | solution.py:78
  147.8 1.1 copy.75
  (113 shorter events, 24.3 us)
Async XLA Ops:
  0.6 83.6 %copy-start = (bf16[256,256]{1,0:T(8,128)(2,1)S(1)}, bf16[256,256]{1,0:T(8,128)(2,1)}, u32[]{:S(2)}) copy-start(bf16[256,256]{1,0:T(8,128)(2,1)} %param.13) | copy-start | bytes 393220
  0.6 9.7 %copy-start.2 = (bf16[256,4,256]{2,1,0:T(4,128)(2,1)S(1)}, bf16[256,4,256]{2,1,0:T(4,128)(2,1)}, u32[]{:S(2)}) copy-start(bf16[256,4,256]{2,1,0:T(4,128)(2,1)} %param.12) | copy-start | bytes 1572868
  3.0 33.0 %all-to-all-start = ((bf16[16,8,16,256]{3,2,0,1:T(8,128)(2,1)}), bf16[16,8,16,256]{3,2,0,1:T(8,128)(2,1)S(1)}, u32[]{:S(2)}, u32[]{:S(2)}) async-start(bf16[16,8,16,256]{3,2,0,1:T(8,128)(2,1)} %copy.61), calls=%async_computation | async-start | bytes 2097152 | tf_op jit(solution)/shard_map/all_to_all | solution.py:51
  38.7 1.7 %copy-start.5 = (f32[256]{0:T(256)S(1)}, f32[256]{0:T(256)}, u32[]{:S(2)}) copy-start(f32[256]{0:T(256)} %param.11) | copy-start | bytes 3076
  55.1 3.0 %copy-start.1 = (bf16[16,128,256]{2,1,0:T(8,128)(2,1)S(1)}, bf16[16,128,256]{2,1,0:T(8,128)(2,1)}, u32[]{:S(2)}) copy-start(bf16[16,128,256]{2,1,0:T(8,128)(2,1)} %custom-call) | copy-start | bytes 3145732
  84.7 5.3 %copy-start.3 = (s32[32,4,16]{0,2,1:T(8,128)S(1)}, s32[32,4,16]{0,2,1:T(8,128)}, u32[]{:S(2)}) copy-start(s32[32,4,16]{0,2,1:T(8,128)} %param.17) | copy-start | bytes 24580
  84.7 5.5 %copy-start.4 = (s32[32,4,16]{0,2,1:T(8,128)S(1)}, s32[32,4,16]{0,2,1:T(8,128)}, u32[]{:S(2)}) copy-start(s32[32,4,16]{0,2,1:T(8,128)} %param.16) | copy-start | bytes 24580
  86.3 17.9 %all-to-all-start.1 = ((bf16[128,1,16,256]{3,2,1,0:T(8,128)(2,1)}), bf16[128,1,16,256]{3,2,1,0:T(8,128)(2,1)S(1)}, u32[]{:S(2)}, u32[]{:S(2)}) async-start(bf16[128,1,16,256]{3,2,1,0:T(8,128)(2,1)} %bitcast.79), calls=%async_computation.1 | async-start | bytes 2097152 | tf_op jit(solution)/shard_map/all_to_all | solution.py:68
  104.8 1.4 copy-start.6
where the time goes:
time: 153 us; the launch traced here: 152 us
  waiting for transfers between devices  39.6 us (26%)
  local copies, waits for them, and re-layouts  38.2 us (25%)
  blocking collectives  37.5 us (25%)
  matrix products  12.7 us (8%)
  starting transfers between devices  11 us (7%)
  other arithmetic  7 us (5%)
  between operations  5.11 us (3%)
    psum x1, blocking collectives, on_device(): loss_sum, mask_count = lax.psum((local_loss, local_count), ('seq', 'res'))  37.5 us
    all_to_all x1, waiting for transfers between devices, on_device(): lax.all_to_all(split_view, 'seq', split_axis=1, concat_axis=0, tiled=True)  25.7 us
    squeeze x16, local copies, waits for them, and re-layouts, on_device(): lax.map(per_column, projected).reshape(col_count * seq_total, features)  15.5 us
    all_to_all x1, waiting for transfers between devices, on_device(): lax.all_to_all(result, 'res', split_axis=0, concat_axis=1, tiled=True)  13.9 us
    all_to_all x1, starting transfers between devices, on_device(): lax.all_to_all(split_view, 'seq', split_axis=1, concat_axis=0, tiled=True)  7.28 us
    convert_element_type x1, local copies, waits for them, and re-layouts, project(): return jnp.dot(normed, w_proj.reshape(features, 4 * features), preferred_...  6.52 us
    dot_general x16, matrix products, column_attention(): jnp.einsum('shd,thd->hst', queries, key_part, preferred_element_type=jnp....  5.03 us
    unnamed x19, local copies, waits for them, and re-layouts  5 us
  transfers between devices with their start and end apart: 2, of which 2 were waited for; matrix products, arithmetic and copies ran while one was open for 0% of the time, Pallas kernels for 0%

commit v1 on v0

v1 whole, which is shorter than its diff:
```python
import functools
import math

import jax
import jax.numpy as jnp
from jax import lax
from jax.experimental import pallas as pl
from jax.experimental.pallas import tpu as pltpu
from jax.sharding import PartitionSpec as P

HEADS = 8
HEAD_DIM = 32
MESH = pl.DeviceIdType.MESH
GROUP = 8
LANES = 128
F32 = jnp.float32
BF16 = jnp.bfloat16


def flip(index, mask):
    bit = 1
    out = index
    while bit <= mask:
        if mask & bit:
            out = out + bit * (1 - 2 * ((index // bit) % 2))
        bit *= 2
    return out


def peer_of(me, step, count):
    if count & (count - 1) == 0:
        return flip(me, step)
    return (me + step) % count


def source_of(me, step, count):
    if count & (count - 1) == 0:
        return flip(me, step)
    return (me + count - step) % count


def layer_norm(values, gain):
    mean = jnp.mean(values, axis=-1, keepdims=True)
    centred = values - mean
    spread = jnp.mean(centred * centred, axis=-1, keepdims=True)
    return centred * lax.rsqrt(spread + 1e-05) * gain


def kernel(
    seq_n, res_n, entries, classes,
    x_hbm, gain_attn, w_proj, w_out, gain_head, w_head, codes_in,
    out_hbm, loss_out, share_out,
    recv, xf, yf, send, ones_bd, codes, part, part2, loss_acc,
    s1, r1, s2, r2, sc, rc, sp, rp, sq, rq, loc, loc2,
):
    rows_local, groups, _, feats = x_hbm.shape
    halves = groups // seq_n
    total = recv.shape[1]
    out_rows = total // res_n
    me_s = lax.axis_index("seq")
    me_r = lax.axis_index("res")
    seq_steps = sorted(range(1, seq_n), reverse=True)

    barrier = pltpu.get_barrier_semaphore()
    for k in range(1, seq_n):
        pl.semaphore_signal(barrier, inc=1, device_id={"seq": peer_of(me_s, k, seq_n), "res": me_r}, device_id_type=MESH)
    for k in range(1, res_n):
        pl.semaphore_signal(barrier, inc=1, device_id={"seq": me_s, "res": peer_of(me_r, k, res_n)}, device_id_type=MESH)
    pl.semaphore_wait(barrier, seq_n + res_n - 2)

    def dest_rows(who):
        return pl.ds(pl.multiple_of(who * rows_local, rows_local), rows_local)

    def exchange1(h, k):
        peer = peer_of(me_s, k, seq_n)
        return pltpu.make_async_remote_copy(
            src_ref=x_hbm.at[:, peer * halves + h],
            dst_ref=recv.at[h, dest_rows(me_s)],
            send_sem=s1.at[h, k], recv_sem=r1.at[h, k],
            device_id={"seq": peer, "res": me_r}, device_id_type=MESH,
        )

    def arrive1(h, k):
        src = source_of(me_s, k, seq_n)
        return pltpu.make_async_remote_copy(
            src_ref=x_hbm.at[:, h],
            dst_ref=recv.at[h, dest_rows(src)],
            send_sem=s1.at[h, k], recv_sem=r1.at[h, k],
            device_id={"seq": src, "res": me_r}, device_id_type=MESH,
        )

    def own1(h):
        return pltpu.make_async_copy(x_hbm.at[:, me_s * halves + h], recv.at[h, dest_rows(me_s)], loc.at[h])

    def code_copy(k):
        peer = peer_of(me_r, k, res_n)
        return pltpu.make_async_remote_copy(
            src_ref=codes_in.at[peer], dst_ref=codes.at[me_r],
            send_sem=sc.at[k], recv_sem=rc.at[k],
            device_id={"seq": me_s, "res": peer}, device_id_type=MESH,
        )

    def code_arrive(k):
        src = source_of(me_r, k, res_n)
        return pltpu.make_async_remote_copy(
            src_ref=codes_in.at[src], dst_ref=codes.at[src],
            send_sem=sc.at[k], recv_sem=rc.at[k],
            device_id={"seq": me_s, "res": src}, device_id_type=MESH,
        )

    for h in range(halves):
        for k in seq_steps:
            exchange1(h, k).start()
        own1(h).start()
    for k in range(1, res_n):
        code_copy(k).start()
    codes[me_r] = codes_in[me_r]

    lane_head = lax.broadcasted_iota(jnp.int32, (total, feats), 1) // HEAD_DIM
    for hd in range(HEADS):
        ones_bd[hd * total:(hd + 1) * total, :] = jnp.where(lane_head == hd, 1.0, 0.0).astype(BF16)
    loss_acc[...] = jnp.zeros_like(loss_acc)
    scale = HEAD_DIM ** (-0.5) * math.log2(math.e)
    q_tile = min(total, 128)
    per = max(1, (8 * 128) // total)

    def column(h, c):
        x = jnp.concatenate([xf[i, pl.ds(c, total, stride=GROUP), :] for i in range(feats // LANES)], axis=1)
        normed = layer_norm(x, gain_attn[...]).astype(BF16)
        q = jnp.dot(normed, w_proj[:, 0:feats], preferred_element_type=F32).astype(BF16)
        key = jnp.dot(normed, w_proj[:, feats:2 * feats], preferred_element_type=F32).astype(BF16)
        val = jnp.dot(normed, w_proj[:, 2 * feats:3 * feats], preferred_element_type=F32).astype(BF16)
        gate = jnp.dot(normed, w_proj[:, 3 * feats:4 * feats], preferred_element_type=F32)
        zero = jnp.zeros((), BF16)
        parts = []
        for q0 in range(0, total, q_tile):
            qt = q[q0:q0 + q_tile]
            acc = None
            tot = None
            for g0 in range(0, HEADS, per):
                hs = range(g0, min(HEADS, g0 + per))
                mine = [ones_bd[hd * total:(hd + 1) * total, :] for hd in hs]
                kbd = jnp.concatenate([key * m for m in mine], axis=0)
                vbd = jnp.concatenate([val * m for m in mine], axis=0)
                scores = lax.dot_general(qt, kbd, (((1,), (1,)), ((), ())), preferred_element_type=F32)
                probs = jnp.exp2(scores * scale).astype(BF16)
                a = jnp.dot(probs, vbd, preferred_element_type=F32)
                t = jnp.dot(probs, ones_bd[hs[0] * total:(hs[-1] + 1) * total, :], preferred_element_type=F32)
                acc = a if acc is None else acc + a
                tot = t if tot is None else tot + t
            parts.append(acc / tot)
        attended = parts[0] if len(parts) == 1 else jnp.concatenate(parts, axis=0)
        gated = (attended * jax.nn.sigmoid(gate)).astype(BF16)
        y = x + jnp.dot(gated, w_out[...], preferred_element_type=F32)
        for i in range(feats // LANES):
            yf[i, pl.ds(c, total, stride=GROUP), :] = y[:, i * LANES:(i + 1) * LANES]

    def res_rows(who):
        return pl.ds(pl.multiple_of(who * out_rows, out_rows), out_rows)

    def exchange2(h, k):
        peer = peer_of(me_r, k, res_n)
        return pltpu.make_async_remote_copy(
            src_ref=send.at[h, res_rows(peer)], dst_ref=out_hbm.at[:, me_r, h],
            send_sem=s2.at[h, k], recv_sem=r2.at[h, k],
            device_id={"seq": me_s, "res": peer}, device_id_type=MESH,
        )

    def arrive2(h, k):
        src = source_of(me_r, k, res_n)
        return pltpu.make_async_remote_copy(
            src_ref=send.at[h, res_rows(src)], dst_ref=out_hbm.at[:, src, h],
            send_sem=s2.at[h, k], recv_sem=r2.at[h, k],
            device_id={"seq": me_s, "res": src}, device_id_type=MESH,
        )

    def own2(h):
        return pltpu.make_async_copy(send.at[h, res_rows(me_r)], out_hbm.at[:, me_r, h], loc2.at[h])

    def attention(h):
        for k in seq_steps:
            arrive1(h, k).wait_recv()
        own1(h).wait()

        def widen(i, carry):
            rows = pl.ds(pl.multiple_of(i * rows_local, rows_local), rows_local)
            flat = pl.ds(pl.multiple_of(i * rows_local * GROUP, rows_local * GROUP), rows_local * GROUP)
            wide = recv[h, rows].astype(F32).reshape(rows_local * GROUP, feats)
            for j in range(feats // LANES):
                xf[j, flat, :] = wide[:, j * LANES:(j + 1) * LANES]
            return carry
        lax.fori_loop(0, total // rows_local, widen, 0)

        def one(c, carry):
            column(h, c)
            return carry
        lax.fori_loop(0, GROUP, one, 0, unroll=2 if total <= 128 else 1)

        def narrow(i, carry):
            rows = pl.ds(pl.multiple_of(i * rows_local, rows_local), rows_local)
            flat = pl.ds(pl.multiple_of(i * rows_local * GROUP, rows_local * GROUP), rows_local * GROUP)
            wide = jnp.concatenate([yf[j, flat, :] for j in range(feats // LANES)], axis=1)
            send[h, rows] = wide.reshape(rows_local, GROUP, feats).astype(BF16)
            return carry
        lax.fori_loop(0, total // rows_local, narrow, 0)
        for k in range(res_n - 1, 0, -1):
            exchange2(h, k).start()
        own2(h).start()

    def head(h):
        kinds = w_head.shape[0]
        width = out_rows * GROUP
        for r in range(res_n):
            rows = send[h, r * out_rows:(r + 1) * out_rows].astype(F32).reshape(width, feats)
            head_in = layer_norm(rows, gain_head[...]).astype(BF16)
            logits = lax.dot_general(w_head[...], head_in, (((1,), (1,)), ((), ())), preferred_element_type=F32)
            kind = lax.broadcasted_iota(jnp.int32, (kinds, width), 0)
            sums = jnp.sum(jnp.where(kind < classes, jnp.exp(logits), 0.0), axis=0, keepdims=True)
            code = codes[r, h]
            picked = jnp.sum(jnp.where(kind == code, logits, 0.0), axis=0, keepdims=True)
            on = code >= 0
            loss_acc[0:1, :] += jnp.where(on, jnp.log(sums) - picked, 0.0)
            loss_acc[1:2, :] += jnp.where(on, 1.0, 0.0)

    for h in range(halves):
        attention(h)
        if h == 0:
            for k in range(1, res_n):
                code_arrive(k).wait_recv()
        head(h)

    def part_copy(k, arriving):
        who = source_of(me_s, k, seq_n) if arriving else peer_of(me_s, k, seq_n)
        return pltpu.make_async_remote_copy(
            src_ref=part.at[0], dst_ref=part.at[k],
            send_sem=sp.at[k], recv_sem=rp.at[k],
            device_id={"seq": who, "res": me_r}, device_id_type=MESH,
        )

    def part2_copy(k, arriving):
        who = source_of(me_r, k, res_n) if arriving else peer_of(me_r, k, res_n)
        return pltpu.make_async_remote_copy(
            src_ref=part2.at[0], dst_ref=part2.at[k],
            send_sem=sq.at[k], recv_sem=rq.at[k],
            device_id={"seq": me_s, "res": who}, device_id_type=MESH,
        )

    width = loss_acc.shape[1]
    mine = loss_acc[:, 0:128]
    for w0 in range(128, width, 128):
        mine = mine + loss_acc[:, w0:w0 + 128]
    part[0] = mine
    for k in seq_steps:
        part_copy(k, False).start()
    for k in seq_steps:
        part_copy(k, True).wait_recv()
    both = part[0]
    for k in range(1, seq_n):
        both = both + part[k]
    part2[0] = both
    for k in range(1, res_n):
        part2_copy(k, False).start()
    for k in range(1, res_n):
        part2_copy(k, True).wait_recv()
    both = part2[0]
    for k in range(1, res_n):
        both = both + part2[k]
    sums = jnp.sum(both, axis=1, keepdims=True)
    loss_out[...] = jnp.broadcast_to(sums[0:1] / (1.0 + sums[1:2]), loss_out.shape)
    share_out[...] = jnp.broadcast_to(sums[1:2] / entries, share_out.shape)

    for h in range(halves):
        for k in range(1, res_n):
            arrive2(h, k).wait_recv()
            exchange2(h, k).wait_send()
        own2(h).wait()
        for k in seq_steps:
            exchange1(h, k).wait_send()
    for k in range(1, res_n):
        code_copy(k).wait_send()
        part2_copy(k, False).wait_send()
    for k in seq_steps:
        part_copy(k, False).wait_send()


def on_device(seq_n, res_n, alignment, gain_attn, w_proj, w_out, gain_head, w_head, masked, labels):
    rows_local, _, segment, feats = alignment.shape
    total = rows_local * seq_n
    cols = segment // seq_n
    halves = cols // GROUP
    out_rows = labels.shape[0]
    classes = w_head.shape[1]
    kinds = -(-classes // 16) * 16
    entries = total * res_n * segment
    x = alignment.reshape(rows_local, segment // GROUP, GROUP, feats)
    code = jnp.where(masked > 0, labels, -1)
    code = code.reshape(out_rows, res_n, halves, GROUP).transpose(1, 2, 0, 3)
    width = out_rows * GROUP
    code = code.reshape(res_n, halves, 1, width)
    head_t = jnp.pad(w_head.T, ((0, kinds - classes), (0, 0)))
    vm = pl.BlockSpec(memory_space=pltpu.VMEM)
    hbm = pl.BlockSpec(memory_space=pl.ANY)
    dma = pltpu.SemaphoreType.DMA
    out, loss, share = pl.pallas_call(
        functools.partial(kernel, seq_n, res_n, float(entries), classes),
        out_shape=(
            jax.ShapeDtypeStruct((out_rows, res_n, halves, GROUP, feats), BF16),
            jax.ShapeDtypeStruct((1, 128), F32),
            jax.ShapeDtypeStruct((1, 128), F32),
        ),
        in_specs=[hbm] + [vm] * 6,
        out_specs=(hbm, vm, vm),
        scratch_shapes=[
            pltpu.VMEM((halves, total, GROUP, feats), BF16),
            pltpu.VMEM((feats // LANES, total * GROUP, LANES), F32),
            pltpu.VMEM((feats // LANES, total * GROUP, LANES), F32),
            pltpu.VMEM((halves, total, GROUP, feats), BF16),
            pltpu.VMEM((HEADS * total, feats), BF16),
            pltpu.VMEM((res_n, halves, 1, width), jnp.int32),
            pltpu.VMEM((seq_n, 8, 128), F32),
            pltpu.VMEM((res_n, 8, 128), F32),
            pltpu.VMEM((8, width), F32),
            dma((halves, seq_n)), dma((halves, seq_n)),
            dma((halves, res_n)), dma((halves, res_n)),
            dma((res_n,)), dma((res_n,)),
            dma((seq_n,)), dma((seq_n,)),
            dma((res_n,)), dma((res_n,)),
            dma((halves,)), dma((halves,)),
        ],
        compiler_params=pltpu.CompilerParams(
            collective_id=0, has_side_effects=True, vmem_limit_bytes=60 * 1024 * 1024
        ),
    )(
        x, gain_attn.reshape(1, feats), w_proj.reshape(feats, 4 * feats), w_out,
        gain_head.reshape(1, feats), head_t, code,
    )
    return out.reshape(out_rows, res_n, cols, feats), loss[0, 0], share[0, 0]


def solution(mesh):
    in_specs = (
        P("seq", "res", None, None),
        P(), P(), P(), P(), P(),
        P("res", None, "seq"),
        P("res", None, "seq"),
    )
    out_specs = (P("res", None, "seq", None), P(), P())
    body = functools.partial(on_device, mesh.shape["seq"], mesh.shape["res"])
    return jax.shard_map(body, mesh=mesh, in_specs=in_specs, out_specs=out_specs, check_vma=False)
```

time: 153 us -> 60.2 us (0.39)
  Pallas kernels: 0 us -> 49.1 us
  waiting for transfers between devices: 39.6 us -> 0 us
  blocking collectives: 37.5 us -> 0 us
  local copies, waits for them, and re-layouts: 38.2 us -> 6.96 us
  matrix products: 12.7 us -> 0 us
  starting transfers between devices: 11 us -> 0 us
  other arithmetic: 7 us -> 0.76 us
  between operations: 5.11 us -> 3 us
    pallas_call x0 -> x1, Pallas kernels: none -> 49.1 us  [on_device(): pl.pallas_call(functools.partial(kernel, seq_n, res_n, float(entries), cl...]
    all_to_all x2 -> x0, waiting for transfers between devices: 39.6 us -> none  [the longest x1 25.7 us: on_device(): lax.all_to_all(split_view, 'seq', split_axis=1, concat_axis=0, tiled=True)]
    psum x1 -> x0, blocking collectives: 37.5 us -> none  [on_device(): loss_sum, mask_count = lax.psum((local_loss, local_count), ('seq', 'res'))]
    squeeze x16 -> x0, local copies, waits for them, and re-layouts: 15.5 us -> none  [on_device(): lax.map(per_column, projected).reshape(col_count * seq_total, features)]
    dot_general x35 -> x0, matrix products: 12.7 us -> none  [the longest x16 5.03 us: column_attention(): jnp.einsum('shd,thd->hst', queries, key_part, preferred_element_type=jnp....]
    all_to_all x2 -> x0, starting transfers between devices: 11 us -> none  [the longest x1 7.28 us: on_device(): lax.all_to_all(split_view, 'seq', split_axis=1, concat_axis=0, tiled=True)]
    convert_element_type x3 -> x0, local copies, waits for them, and re-layouts: 8.03 us -> none  [the longest x1 6.52 us: project(): return jnp.dot(normed, w_proj.reshape(features, 4 * features), preferred_...]
    reduce_sum x5 -> x0, other arithmetic: 4.43 us -> none  [the longest x2 2.27 us: normalize(): spread = jnp.mean(centred * centred, axis=-1, keepdims=True)]
  transfers between devices with their start and end apart: 2 -> 0, of which waited for: 2 -> 0; matrix products, arithmetic and copies ran while one was open for 0% -> 0% of each run, Pallas kernels for 0% -> 0%
where the time goes in v1:
time: 60.2 us; the launch traced here: 59.9 us
  Pallas kernels  49.1 us (82%)
  local copies, waits for them, and re-layouts  6.96 us (12%)
  between operations  3 us (5%)
  other arithmetic  0.76 us (1%)
    pallas_call x1, Pallas kernels, on_device(): pl.pallas_call(functools.partial(kernel, seq_n, res_n, float(entries), cl...  49.1 us
    unnamed x8, local copies, waits for them, and re-layouts  4.82 us
    pad x1, local copies, waits for them, and re-layouts, on_device(): head_t = jnp.pad(w_head.T, ((0, kinds - classes), (0, 0)))  1.33 us

profile of v1, /device:TPU:0, one launch (start us, length us, event | category | flops | bytes accessed | tf_op | source)
XLA Modules:
  0.0 59.9 jit_solution(17821099197798480346)
XLA Ops:
  0.6 0.0 copy-start
  0.6 1.3 %pad.4.w_head = bf16[32,256]{1,0:T(8,128)(2,1)} pad(bf16[23,256]{1,0:T(8,128)(2,1)} %bitcast.21, bf16[]{:T(256)} %constant.1.clone.1), padding=0_9x0_0 | pad | bytes 28162 | tf_op jit(solution)/shard_map/jit(_pad)/pad | solution.py:300
  2.0 0.0 copy-done
  2.0 0.8 %select_bitcast_fusion = s32[32,4,2,8]{0,3,2,1:T(8,128)S(1)} fusion(s32[32,4,16]{0,2,1:T(8,128)S(1)} %copy-done, s32[32,4,16]{0,2,1:T(8,128)} %param.14), kind=kLoop, calls=%fused_computation | loop fusion | flops 4096 | bytes 24576 | tf_op jit(solution)/shard_map/reshape | solution.py:297
  2.7 0.1 copy.12
  2.8 0.7 %reshape.34.codes_in = s32[4,2,1,256]{3,2,1,0:T(1,128)} reshape(s32[4,2,32,8]{3,2,1,0:T(8,128)S(1)} %bitcast.19) | data formatting | bytes 16384 | tf_op jit(solution)/shard_map/reshape | solution.py:299
  3.5 1.9 %copy.14 = bf16[32,8,4,256]{3,1,2,0:T(8,128)(2,1)} copy(bf16[32,8,4,256]{3,2,1,0:T(4,128)(2,1)} %bitcast.20) | data formatting | bytes 1048576
  5.5 49.1 %shard_map.103 = (bf16[32,4,2,8,256]{4,3,2,1,0:T(8,128)(2,1)}, f32[1,128]{1,0:T(1,128)}, f32[1,128]{1,0:T(1,128)}) custom-call(bf16[16,16,8,256]{3,2,1,0:T(8,128)(2,1)} %bitcast.17, f32[1,256]{1,0:T(1,128)} %bitcast.22, bf16[256,1024]{1,0:T(8,128)(2,1)} %bitcast.16, bf16[256,256]{1,0:T(8,128)(2,1)} %w_out.1, f32[1,256]{1,0:T(1,128)} %bitcast.23, ...), custom_call_target="tpu_custom_call" | custom-call | tf_op jit(solution)/shard_map/pallas_call | solution.py:304
  54.6 0.0 copy-start.2
  54.6 2.3 %copy.18 = bf16[32,4,16,256]{3,2,1,0:T(8,128)(2,1)} copy(bf16[32,4,16,256]{3,2,1,0:T(8,128)(2,1)} %bitcast.18) | data formatting | bytes 2097152
  56.9 0.0 copy-done.2
  56.9 0.0 copy-start.1
  57.0 0.6 copy-done.1
Async XLA Ops:
  0.6 1.3 %copy-start = (s32[32,4,16]{0,2,1:T(8,128)S(1)}, s32[32,4,16]{0,2,1:T(8,128)}, u32[]{:S(2)}) copy-start(s32[32,4,16]{0,2,1:T(8,128)} %param.15) | copy-start | bytes 24580
  54.6 2.3 %copy-start.2 = (f32[1,128]{1,0:T(1,128)S(1)}, f32[1,128]{1,0:T(1,128)}, u32[]{:S(2)}) copy-start(f32[1,128]{1,0:T(1,128)} %get-tuple-element.7) | copy-start | bytes 1540
  56.9 0.6 %copy-start.1 = (f32[1,128]{1,0:T(1,128)S(1)}, f32[1,128]{1,0:T(1,128)}, u32[]{:S(2)}) copy-start(f32[1,128]{1,0:T(1,128)} %get-tuple-element.8) | copy-start | bytes 1540

commit v2 on v1

--- a/solution.py
+++ b/solution.py
@@ -47,11 +47,11 @@
 
 
 def kernel(
-    seq_n, res_n, entries, classes,
-    x_hbm, gain_attn, w_proj, w_out, gain_head, w_head, codes_in,
+    seq_n, res_n, entries,
+    x_hbm, gain_attn, w_proj_hbm, w_out_hbm, gain_head, w_head, masked, labels,
     out_hbm, loss_out, share_out,
-    recv, xf, yf, send, ones_bd, codes, part, part2, loss_acc,
-    s1, r1, s2, r2, sc, rc, sp, rp, sq, rq, loc, loc2,
+    recv, xf, yb, pf, send, perm, ones_bd, w_raw, w_wide, w_proj, w_out, codes_in, codes, code_all, part, part2, loss_acc,
+    s1, r1, s2, r2, sc, rc, sp, rp, sq, rq, loc, loc2, wsem,
 ):
     rows_local, groups, _, feats = x_hbm.shape
     halves = groups // seq_n
@@ -112,26 +112,62 @@
         for k in seq_steps:
             exchange1(h, k).start()
         own1(h).start()
+    w_copy = pltpu.make_async_copy(w_proj_hbm, w_raw, wsem.at[0])
+    wo_copy = pltpu.make_async_copy(w_out_hbm, w_out, wsem.at[1])
+    w_copy.start()
+    wo_copy.start()
+
+    code = jnp.where(masked[...] > 0, labels[...], -1)
+    spread = [jnp.where(me_r == i, code, -1) for i in range(res_n)]
+    codes_in[...] = jnp.concatenate(spread, axis=2)
+    loss_acc[...] = jnp.zeros_like(loss_acc)
+
+    w_copy.wait()
+    wo_copy.wait()
+    lanes = feats // LANES
+    step_rows = 64
+    for r0 in range(0, feats, step_rows):
+        wide = w_raw[r0:r0 + step_rows].astype(F32)
+        for j in range(lanes):
+            w_wide[j, r0:r0 + step_rows, 0:4, :] = wide[:, :, j * LANES:(j + 1) * LANES]
+    for j in range(lanes):
+        flat = w_wide.at[j].reshape(feats * 8, LANES)
+        for b in range(4):
+            w_proj[:, b * feats + j * LANES:b * feats + (j + 1) * LANES] = flat[pl.ds(b, feats, stride=8), :].astype(BF16)
+
     for k in range(1, res_n):
         code_copy(k).start()
-    codes[me_r] = codes_in[me_r]
-
+
+    scale = HEAD_DIM ** (-0.5) * math.log2(math.e)
+    q_tile = min(total, 128)
+    per = max(1, (8 * 128) // total)
     lane_head = lax.broadcasted_iota(jnp.int32, (total, feats), 1) // HEAD_DIM
     for hd in range(HEADS):
         ones_bd[hd * total:(hd + 1) * total, :] = jnp.where(lane_head == hd, 1.0, 0.0).astype(BF16)
-    loss_acc[...] = jnp.zeros_like(loss_acc)
-    scale = HEAD_DIM ** (-0.5) * math.log2(math.e)
-    q_tile = min(total, 128)
-    per = max(1, (8 * 128) // total)
+
+    block = rows_local * GROUP
+    first = lax.broadcasted_iota(jnp.int32, (block, block), 0)
+    second = lax.broadcasted_iota(jnp.int32, (block, block), 1)
+    there = (second % GROUP == first // rows_local) & (second // GROUP == first % rows_local)
+    back = (first % GROUP == second // rows_local) & (first // GROUP == second % rows_local)
+    perm[0] = jnp.where(there, 1.0, 0.0).astype(BF16)
+    perm[1] = jnp.where(back, 1.0, 0.0).astype(BF16)
+
+    def ingest(h, src):
+        rows = dest_rows(src)
+        came = recv[h, rows].reshape(block, feats)
+        wide = jnp.dot(perm[0], came, preferred_element_type=F32)
+        xf[:, rows, :] = wide.reshape(GROUP, rows_local, feats)
+        normed = layer_norm(wide, gain_attn[...]).astype(BF16)
+        made = jnp.dot(normed, w_proj[...], preferred_element_type=F32)
+        pf[:, rows, :] = made.astype(BF16).reshape(GROUP, rows_local, 4 * feats)
 
     def column(h, c):
-        x = jnp.concatenate([xf[i, pl.ds(c, total, stride=GROUP), :] for i in range(feats // LANES)], axis=1)
-        normed = layer_norm(x, gain_attn[...]).astype(BF16)
-        q = jnp.dot(normed, w_proj[:, 0:feats], preferred_element_type=F32).astype(BF16)
-        key = jnp.dot(normed, w_proj[:, feats:2 * feats], preferred_element_type=F32).astype(BF16)
-        val = jnp.dot(normed, w_proj[:, 2 * feats:3 * feats], preferred_element_type=F32).astype(BF16)
-        gate = jnp.dot(normed, w_proj[:, 3 * feats:4 * feats], preferred_element_type=F32)
-        zero = jnp.zeros((), BF16)
+        x = xf[c]
+        q = pf[c, :, 0:feats]
+        key = pf[c, :, feats:2 * feats]
+        val = pf[c, :, 2 * feats:3 * feats]
+        gate = pf[c, :, 3 * feats:4 * feats].astype(F32)
         parts = []
         for q0 in range(0, total, q_tile):
             qt = q[q0:q0 + q_tile]
@@ -152,8 +188,7 @@
         attended = parts[0] if len(parts) == 1 else jnp.concatenate(parts, axis=0)
         gated = (attended * jax.nn.sigmoid(gate)).astype(BF16)
         y = x + jnp.dot(gated, w_out[...], preferred_element_type=F32)
-        for i in range(feats // LANES):
-            yf[i, pl.ds(c, total, stride=GROUP), :] = y[:, i * LANES:(i + 1) * LANES]
+        yb[c] = y.astype(BF16)
 
     def res_rows(who):
         return pl.ds(pl.multiple_of(who * out_rows, out_rows), out_rows)
@@ -178,55 +213,65 @@
         return pltpu.make_async_copy(send.at[h, res_rows(me_r)], out_hbm.at[:, me_r, h], loc2.at[h])
 
     def attention(h):
-        for k in seq_steps:
-            arrive1(h, k).wait_recv()
         own1(h).wait()
-
-        def widen(i, carry):
-            rows = pl.ds(pl.multiple_of(i * rows_local, rows_local), rows_local)
-            flat = pl.ds(pl.multiple_of(i * rows_local * GROUP, rows_local * GROUP), rows_local * GROUP)
-            wide = recv[h, rows].astype(F32).reshape(rows_local * GROUP, feats)
-            for j in range(feats // LANES):
-                xf[j, flat, :] = wide[:, j * LANES:(j + 1) * LANES]
-            return carry
-        lax.fori_loop(0, total // rows_local, widen, 0)
+        if seq_n <= 8:
+            ingest(h, me_s)
+            near = [k for k in seq_steps if 2 * k < seq_n]
+            for k in near[::-1] + [k for k in seq_steps if 2 * k >= seq_n]:
+                arrive1(h, k).wait_recv()
+                ingest(h, source_of(me_s, k, seq_n))
+        else:
+            for k in seq_steps:
+                arrive1(h, k).wait_recv()
+
+            def take_in(i, carry):
+                ingest(h, i)
+                return carry
+            lax.fori_loop(0, seq_n, take_in, 0)
 
         def one(c, carry):
             column(h, c)
             return carry
-        lax.fori_loop(0, GROUP, one, 0, unroll=2 if total <= 128 else 1)
+        lax.fori_loop(0, GROUP, one, 0, unroll=4 if total <= 128 else 1)
 
         def narrow(i, carry):
             rows = pl.ds(pl.multiple_of(i * rows_local, rows_local), rows_local)
-            flat = pl.ds(pl.multiple_of(i * rows_local * GROUP, rows_local * GROUP), rows_local * GROUP)
-            wide = jnp.concatenate([yf[j, flat, :] for j in range(feats // LANES)], axis=1)
+            wide = jnp.dot(perm[1], yb[:, rows, :].reshape(block, feats), preferred_element_type=F32)
             send[h, rows] = wide.reshape(rows_local, GROUP, feats).astype(BF16)
             return carry
-        lax.fori_loop(0, total // rows_local, narrow, 0)
+        lax.fori_loop(0, total // rows_local, narrow, 0, unroll=2)
         for k in range(res_n - 1, 0, -1):
             exchange2(h, k).start()
         own2(h).start()
 
     def head(h):
         kinds = w_head.shape[0]
-        width = out_rows * GROUP
-        for r in range(res_n):
-            rows = send[h, r * out_rows:(r + 1) * out_rows].astype(F32).reshape(width, feats)
+
+        def one(c, carry):
+            loss, count = carry
+            rows = yb[c].astype(F32)
             head_in = layer_norm(rows, gain_head[...]).astype(BF16)
             logits = lax.dot_general(w_head[...], head_in, (((1,), (1,)), ((), ())), preferred_element_type=F32)
-            kind = lax.broadcasted_iota(jnp.int32, (kinds, width), 0)
-            sums = jnp.sum(jnp.where(kind < classes, jnp.exp(logits), 0.0), axis=0, keepdims=True)
-            code = codes[r, h]
+            kind = lax.broadcasted_iota(jnp.int32, (kinds, total), 0)
+            sums = jnp.sum(jnp.exp(logits), axis=0, keepdims=True)
+            code = code_all[pl.ds(h * GROUP + c, 1), :]
             picked = jnp.sum(jnp.where(kind == code, logits, 0.0), axis=0, keepdims=True)
             on = code >= 0
-            loss_acc[0:1, :] += jnp.where(on, jnp.log(sums) - picked, 0.0)
-            loss_acc[1:2, :] += jnp.where(on, 1.0, 0.0)
+            return loss + jnp.where(on, jnp.log(sums) - picked, 0.0), count + jnp.where(on, 1.0, 0.0)
+        zero = jnp.zeros((1, total), F32)
+        loss, count = lax.fori_loop(0, GROUP, one, (zero, zero), unroll=2)
+        loss_acc[0:1, :] += loss
+        loss_acc[1:2, :] += count
 
     for h in range(halves):
         attention(h)
         if h == 0:
             for k in range(1, res_n):
                 code_arrive(k).wait_recv()
+            mix = codes_in[me_r]
+            for k in range(1, res_n):
+                mix = jnp.maximum(mix, codes[source_of(me_r, k, res_n)])
+            code_all[...] = mix
         head(h)
 
     def part_copy(k, arriving):
@@ -289,50 +334,51 @@
     cols = segment // seq_n
     halves = cols // GROUP
     out_rows = labels.shape[0]
-    classes = w_head.shape[1]
-    kinds = -(-classes // 16) * 16
     entries = total * res_n * segment
     x = alignment.reshape(rows_local, segment // GROUP, GROUP, feats)
-    code = jnp.where(masked > 0, labels, -1)
-    code = code.reshape(out_rows, res_n, halves, GROUP).transpose(1, 2, 0, 3)
-    width = out_rows * GROUP
-    code = code.reshape(res_n, halves, 1, width)
-    head_t = jnp.pad(w_head.T, ((0, kinds - classes), (0, 0)))
     vm = pl.BlockSpec(memory_space=pltpu.VMEM)
     hbm = pl.BlockSpec(memory_space=pl.ANY)
     dma = pltpu.SemaphoreType.DMA
     out, loss, share = pl.pallas_call(
-        functools.partial(kernel, seq_n, res_n, float(entries), classes),
+        functools.partial(kernel, seq_n, res_n, float(entries)),
         out_shape=(
             jax.ShapeDtypeStruct((out_rows, res_n, halves, GROUP, feats), BF16),
             jax.ShapeDtypeStruct((1, 128), F32),
             jax.ShapeDtypeStruct((1, 128), F32),
         ),
-        in_specs=[hbm] + [vm] * 6,
+        in_specs=[hbm, vm, hbm, hbm, vm, vm, vm, vm],
         out_specs=(hbm, vm, vm),
         scratch_shapes=[
             pltpu.VMEM((halves, total, GROUP, feats), BF16),
-            pltpu.VMEM((feats // LANES, total * GROUP, LANES), F32),
-            pltpu.VMEM((feats // LANES, total * GROUP, LANES), F32),
+            pltpu.VMEM((GROUP, total, feats), F32),
+            pltpu.VMEM((GROUP, total, feats), BF16),
+            pltpu.VMEM((GROUP, total, 4 * feats), BF16),
             pltpu.VMEM((halves, total, GROUP, feats), BF16),
+            pltpu.VMEM((2, rows_local * GROUP, rows_local * GROUP), BF16),
             pltpu.VMEM((HEADS * total, feats), BF16),
-            pltpu.VMEM((res_n, halves, 1, width), jnp.int32),
+            pltpu.VMEM(w_proj.shape, BF16),
+            pltpu.VMEM((feats // LANES, feats, 8, LANES), F32),
+            pltpu.VMEM((feats, 4 * feats), BF16),
+            pltpu.VMEM((feats, feats), BF16),
+            pltpu.VMEM((res_n, cols, total), jnp.int32),
+            pltpu.VMEM((res_n, cols, total), jnp.int32),
+            pltpu.VMEM((cols, total), jnp.int32),
             pltpu.VMEM((seq_n, 8, 128), F32),
             pltpu.VMEM((res_n, 8, 128), F32),
-            pltpu.VMEM((8, width), F32),
+            pltpu.VMEM((8, total), F32),
             dma((halves, seq_n)), dma((halves, seq_n)),
             dma((halves, res_n)), dma((halves, res_n)),
             dma((res_n,)), dma((res_n,)),
             dma((seq_n,)), dma((seq_n,)),
             dma((res_n,)), dma((res_n,)),
-            dma((halves,)), dma((halves,)),
+            dma((halves,)), dma((halves,)), dma((2,)),
         ],
         compiler_params=pltpu.CompilerParams(
             collective_id=0, has_side_effects=True, vmem_limit_bytes=60 * 1024 * 1024
         ),
     )(
-        x, gain_attn.reshape(1, feats), w_proj.reshape(feats, 4 * feats), w_out,
-        gain_head.reshape(1, feats), head_t, code,
+        x, gain_attn.reshape(1, feats), w_proj, w_out, gain_head.reshape(1, feats), w_head.T,
+        masked.transpose(1, 2, 0), labels.transpose(1, 2, 0),
     )
     return out.reshape(out_rows, res_n, cols, feats), loss[0, 0], share[0, 0]
 

time: 60.2 us -> 56.8 us (0.944)
  local copies, waits for them, and re-layouts: 6.96 us -> 2.84 us
  Pallas kernels: 49.1 us -> 50.7 us
  other arithmetic: 0.76 us -> 0 us
    unnamed x8 -> x5, local copies, waits for them, and re-layouts: 4.82 us -> 2.84 us
    pallas_call x1, Pallas kernels: 49.1 us -> 50.7 us  [on_device(): pl.pallas_call(functools.partial(kernel, seq_n, res_n, float(entries)), o...]
    pad x1 -> x0, local copies, waits for them, and re-layouts: 1.33 us -> none  [on_device(): head_t = jnp.pad(w_head.T, ((0, kinds - classes), (0, 0)))]
    reshape x2 -> x0, local copies, waits for them, and re-layouts: 0.81 us -> none  [the longest x1 0.72 us: on_device(): code = code.reshape(res_n, halves, 1, width)]
    reshape x1 -> x0, other arithmetic: 0.76 us -> none  [on_device(): code = code.reshape(out_rows, res_n, halves, GROUP).transpose(1, 2, 0, 3)]
where the time goes in v2:
time: 56.8 us; the launch traced here: 56.6 us
  Pallas kernels  50.7 us (89%)
  between operations  2.99 us (5%)
  local copies, waits for them, and re-layouts  2.84 us (5%)
    pallas_call x1, Pallas kernels, on_device(): pl.pallas_call(functools.partial(kernel, seq_n, res_n, float(entries)), o...  50.7 us
    unnamed x5, local copies, waits for them, and re-layouts  2.84 us

profile of v2, /device:TPU:0, one launch (start us, length us, event | category | flops | bytes accessed | tf_op | source)
XLA Modules:
  0.0 56.6 jit_solution(14775697650171016678)
XLA Ops:
  0.6 50.7 %shard_map.103 = (bf16[32,4,2,8,256]{4,3,2,1,0:T(8,128)(2,1)}, f32[1,128]{1,0:T(1,128)}, f32[1,128]{1,0:T(1,128)}) custom-call(bf16[16,16,8,256]{3,2,1,0:T(8,128)(2,1)} %bitcast.11, f32[1,256]{1,0:T(1,128)} %bitcast.16, bf16[256,4,256]{2,1,0:T(4,128)(2,1)} %w_proj_hbm.1, bf16[256,256]{1,0:T(8,128)(2,1)} %w_out_hbm.1, f32[1,256]{1,0:T(1,128)} %bitcast.17, ...), custom_call_target="tpu_custom_call" | custom-call | tf_op jit(solution)/shard_map/pallas_call | solution.py:342
  51.4 0.0 copy-start.1
  51.4 2.3 %copy.14 = bf16[32,4,16,256]{3,2,1,0:T(8,128)(2,1)} copy(bf16[32,4,16,256]{3,2,1,0:T(8,128)(2,1)} %bitcast.12) | data formatting | bytes 2097152
  53.7 0.0 copy-done.1
  53.7 0.0 copy-start
  53.7 0.5 copy-done
Async XLA Ops:
  51.4 2.3 %copy-start.1 = (f32[1,128]{1,0:T(1,128)S(1)}, f32[1,128]{1,0:T(1,128)}, u32[]{:S(2)}) copy-start(f32[1,128]{1,0:T(1,128)} %get-tuple-element.7) | copy-start | bytes 1540
  53.7 0.6 %copy-start = (f32[1,128]{1,0:T(1,128)S(1)}, f32[1,128]{1,0:T(1,128)}, u32[]{:S(2)}) copy-start(f32[1,128]{1,0:T(1,128)} %get-tuple-element.8) | copy-start | bytes 1540
